TPU v7x, 128 devices: a whole 4x4x4 slice. The times are simulated.
128 devices in a mesh: row: 8 (over y, core), col: 4 (over z), mp: 4 (over x).
Axes of the slice: x: 4, y: 4, z: 4, core: 2. Of those that a mesh axis runs over, the one named last changes fastest.
Arguments:
- hidden: bfloat16 [32768, 3584], P(('row', 'col'), 'mp'), may hold values from -6 to 6
- old_logp: float32 [32768], P(('row', 'col')), may hold values from -0.6 to 0.6
- rewards: float32 [256], P(('row', 'col')), may hold values from -4 to 4
- resp_dest: int32 [256], P(('row', 'col')), may hold values from 0 to 31, as said below
- resp_len: int32 [256], P(('row', 'col')), may hold values from 1 to 128, as said below
- resp_offset: int32 [256], P(('row', 'col')), may hold values from 0 to 511, as said below
- prompt_group: int32 [256], P(('row', 'col')), may hold values from 0 to 31, as said below
- attn_gain: bfloat16 [3584], replicated, may hold values from 0.099609375 to 1.8984375
- w_query: bfloat16 [3584, 3584], P(None, 'mp'), may hold values from -0.09375 to 0.09375
- q_bias: bfloat16 [3584], P('mp'), may hold values from -3 to 3
- w_key: bfloat16 [3584, 512], P(None, 'mp'), may hold values from -0.09375 to 0.09375
- k_bias: bfloat16 [512], P('mp'), may hold values from -6 to 6
- w_value: bfloat16 [3584, 512], P(None, 'mp'), may hold values from -0.09375 to 0.09375
- v_bias: bfloat16 [512], P('mp'), may hold values from -3 to 3
- w_out: bfloat16 [3584, 3584], P('mp'), may hold values from -0.5 to 0.5
- final_gain: bfloat16 [3584], replicated, may hold values from 0.099609375 to 1.8984375
- chosen_rows: bfloat16 [16384, 3584], P(('row', 'col', 'mp')), may hold values from -0.01171875 to 0.01171875
- log_normalizer: float32 [16384], P(('row', 'col', 'mp')), may hold values from -0.6 to 0.6
Outputs:
- objective: float32 [16384], P(('row', 'col', 'mp'))
- loss: float32 [], replicated
Inputs may be any that keep to these rules, and one draw needn't show every extreme that they name: `resp_dest`: ranks are numbered row index * 4 + col index. A rank's responses go to ranks of the same col index: exactly 1 of them to each such rank, itself included; so every rank receives exactly 8 responses. `resp_len`: the responses bound for one rank hold at most 512 tokens together; in every draw some rank's responses fill all 512 positions, and some response has exactly 128. `resp_offset`: responses bound for one rank lie end to end from position 0, without gaps or intersection. `prompt_group`: each of the 32 groups has exactly 8 responses.
All inputs are finite; a program needn't handle non-finite values.
Results may differ from a plain program's by a relative error of at most 0.0019.
Values may be sent and summed in bfloat16 or wider, within the bound.
No kernel may reach another device: no remote copies, remote signals or barrier semaphores. Data moves between devices by JAX's collectives and lax.ppermute only.
A program may use at most 128 MiB of HBM per device.

v0:
```python
import jax
import jax.numpy as jnp
from jax import lax
from jax.sharding import Mesh
from jax.sharding import PartitionSpec as P

HEAD = 128
GROUP_SIZE = 8
ROW = ("row_0", "row_1")
ROW_COL = ("row_0", "row_1", "col")
ROW_COL_MP = ("row_0", "row_1", "col", "mp")
norm_eps = 1e-06
rope_theta = 1000000.0
clip_low = 0.2
clip_high = 0.28
std_floor = 1.0
mask_fill = -1e30


def sent_to_all(value, axis):
    copies = jnp.broadcast_to(value, (lax.axis_size(axis), *value.shape))
    return lax.all_to_all(copies, axis, split_axis=0, concat_axis=0, tiled=True)


def of_everyone(value, axis):
    everything = sent_to_all(value, axis)
    return jnp.sum(everything, axis=0)


def together(arrays, axis):
    ends = [0]
    for a in arrays:
        ends.append(ends[-1] + a.size)
    total = of_everyone(jnp.concatenate([a.ravel() for a in arrays]), axis)
    return tuple((total[b:e].reshape(a.shape) for a, b, e in zip(arrays, ends, ends[1:])))


def over_axes(value, axes):
    for axis in axes:
        value = lax.psum(value, axis)
    return value


def rotary(matrix, positions):
    half_size = matrix.shape[-1] // 2
    exponents = jnp.arange(half_size, dtype=jnp.float32) * (2.0 / matrix.shape[-1])
    frequency = rope_theta ** (-exponents)
    angles = positions[:, None] * frequency[None, :]
    cosine_table = jnp.cos(angles)[:, None, :]
    sine_table = jnp.sin(angles)[:, None, :]
    first_half = matrix[..., :half_size]
    second_half = matrix[..., half_size:]
    return jnp.concatenate(
        [
            first_half * cosine_table - second_half * sine_table,
            second_half * cosine_table + first_half * sine_table,
        ],
        -1,
    )


def body(
    hidden,
    old_logp,
    rewards,
    resp_dest,
    resp_len,
    resp_offset,
    prompt_group,
    attn_gain,
    w_query,
    q_bias,
    w_key,
    k_bias,
    w_value,
    v_bias,
    w_out,
    final_gain,
    chosen_rows,
    log_normalizer,
):
    highest = lax.Precision.HIGHEST
    row_ranks = lax.axis_size(ROW)
    col_ranks = lax.axis_size("col")
    rank_count = row_ranks * col_ranks
    response_count = resp_dest.shape[0]
    per_peer = response_count // row_ranks
    group_count = rank_count * response_count // GROUP_SIZE
    slot_length = hidden.shape[0] // response_count
    feature_count = hidden.shape[1]
    pack_length = response_count * slot_length // 2
    shard_count = lax.axis_size("mp")
    row_count = pack_length // shard_count
    slot_iota = jnp.arange(response_count, dtype=jnp.int32)
    group_iota = jnp.arange(group_count, dtype=jnp.int32)
    dest_row = resp_dest // col_ranks
    earlier = (slot_iota[None, :] < slot_iota[:, None]) & (dest_row[None, :] == dest_row[:, None])
    slot_in_peer = jnp.sum(earlier.astype(jnp.int32), 1)
    send_slot = dest_row * per_peer + slot_in_peer
    selector = send_slot[None, :] == slot_iota[:, None]
    selector_wide = selector.astype(jnp.float32)
    send_rows = jnp.dot(
        selector.astype(jnp.bfloat16),
        hidden.reshape(response_count, slot_length * feature_count),
        preferred_element_type=jnp.float32,
    ).astype(jnp.bfloat16)
    send_rows = send_rows.reshape(row_ranks, per_peer * slot_length, feature_count)
    send_logp = jnp.dot(
        selector_wide, old_logp.reshape(response_count, slot_length), precision=highest
    )
    send_length = jnp.dot(selector_wide, resp_len.astype(jnp.float32), precision=highest)
    send_offset = jnp.dot(selector_wide, resp_offset.astype(jnp.float32), precision=highest)
    member = (prompt_group[:, None] == group_iota[None, :]).astype(jnp.float32)
    send_info = jnp.stack(
        [
            send_length,
            send_offset,
            jnp.dot(selector_wide, rewards, precision=highest),
            jnp.dot(selector_wide, prompt_group.astype(jnp.float32), precision=highest),
        ],
        1,
    )
    send_info = send_info.reshape(row_ranks, per_peer, send_info.shape[1])
    recv_rows = lax.all_to_all(send_rows, ROW, split_axis=0, concat_axis=0, tiled=True)
    recv_logp, recv_info = (
        lax.all_to_all(send_logp, ROW, split_axis=0, concat_axis=0, tiled=True),
        lax.all_to_all(send_info, ROW, split_axis=0, concat_axis=0, tiled=True),
    )
    recv_info = recv_info.reshape(response_count, recv_info.shape[2])
    lengths = recv_info[:, 0].astype(jnp.int32)
    offsets = recv_info[:, 1].astype(jnp.int32)
    slots = jnp.arange(pack_length, dtype=jnp.int32)[:, None]
    covered = (slots >= offsets[None, :]) & (slots < (offsets + lengths)[None, :])
    occupied = jnp.any(covered, 1)
    within_all = slots - offsets[None, :]
    token_index = jnp.sum(jnp.where(covered, slot_iota[None, :] * slot_length + within_all, 0), 1)
    positions = jnp.sum(jnp.where(covered, within_all, 0), 1).astype(jnp.float32)
    segment = jnp.where(occupied, jnp.sum(jnp.where(covered, slot_iota[None, :], 0), 1), -1)
    flat_rows = recv_rows.reshape(-1, feature_count)
    packed = jnp.where(occupied[:, None], flat_rows[token_index], jnp.zeros((), jnp.bfloat16))
    gathered = lax.all_gather(packed, "mp", axis=1, tiled=True)
    inverse = lax.rsqrt(
        jnp.mean(jnp.square(gathered.astype(jnp.float32)), -1, keepdims=True) + norm_eps
    )
    normed = (gathered.astype(jnp.float32) * inverse * attn_gain.astype(jnp.float32)).astype(
        jnp.bfloat16
    )
    heads_local = w_query.shape[1] // HEAD
    key_heads = w_key.shape[1] // HEAD
    queries = jnp.dot(normed, w_query, preferred_element_type=jnp.float32) + q_bias.astype(
        jnp.float32
    )
    queries = rotary(queries.reshape(pack_length, heads_local, HEAD), positions).astype(
        jnp.bfloat16
    )
    key_rows = jnp.dot(normed, w_key, preferred_element_type=jnp.float32) + k_bias.astype(
        jnp.float32
    )
    key_rows = rotary(key_rows.reshape(pack_length, key_heads, HEAD), positions).astype(
        jnp.bfloat16
    )
    value_rows = (
        (jnp.dot(normed, w_value, preferred_element_type=jnp.float32) + v_bias.astype(jnp.float32))
        .astype(jnp.bfloat16)
        .reshape(pack_length, key_heads, HEAD)
    )
    grouped = queries.reshape(pack_length, key_heads, heads_local // key_heads, HEAD)
    block_size = min(512, pack_length)
    scores = jnp.einsum(
        "qkgd,ekd->kgqe", grouped, key_rows, preferred_element_type=jnp.float32
    ) * HEAD ** (-0.5)
    allowed = (segment[0:block_size, None] == segment[None, :block_size]) & (
        jnp.arange(block_size)[None, :] <= jnp.arange(0, block_size)[:, None]
    )
    scores = jnp.where(allowed, scores, mask_fill)
    highest_score = jnp.max(scores, -1, keepdims=True)
    exponent = jnp.exp(scores - highest_score)
    weights = (exponent / jnp.sum(exponent, -1, keepdims=True)).astype(jnp.bfloat16)
    block_out = jnp.einsum(
        "kgqe,ekd->qkgd", weights, value_rows, preferred_element_type=jnp.float32
    )
    pieces = block_out.reshape(block_size, heads_local * HEAD).astype(jnp.bfloat16)
    branch = lax.psum_scatter(
        jnp.dot(pieces, w_out, preferred_element_type=jnp.float32).astype(jnp.bfloat16),
        "mp",
        scatter_dimension=0,
        tiled=True,
    ).astype(jnp.float32)
    own_start = lax.axis_index("mp") * row_count
    residual = lax.dynamic_slice_in_dim(gathered, own_start, row_count, 0)
    residual_out = (residual.astype(jnp.float32) + branch).astype(jnp.bfloat16)
    final_rows = residual_out.astype(jnp.float32)
    final_inverse = lax.rsqrt(jnp.mean(final_rows * final_rows, -1, keepdims=True) + norm_eps)
    logits = jnp.sum(
        final_rows
        * final_inverse
        * final_gain.astype(jnp.float32)
        * chosen_rows.astype(jnp.float32),
        -1,
    )
    own_covered = lax.dynamic_slice_in_dim(covered, own_start, row_count, 0)
    own_occupied = lax.dynamic_slice_in_dim(occupied, own_start, row_count, 0)
    own_token = lax.dynamic_slice_in_dim(token_index, own_start, row_count, 0)
    own_old = jnp.where(own_occupied, recv_logp.reshape(-1)[own_token], 0.0)
    totals, squares = together(
        (
            jnp.dot(rewards, member, precision=highest),
            jnp.dot(rewards * rewards, member, precision=highest),
        ),
        ROW_COL,
    )
    means = totals / GROUP_SIZE
    variance = jnp.maximum(squares / GROUP_SIZE - means * means, 0.0)
    means, scales = (means, jnp.maximum(jnp.sqrt(variance), std_floor))
    pair_member = (recv_info[:, 3].astype(jnp.int32)[:, None] == group_iota[None, :]).astype(
        jnp.float32
    )
    pair_adv = (recv_info[:, 2] - jnp.dot(pair_member, means, precision=highest)) / jnp.dot(
        pair_member, scales, precision=highest
    )
    token_adv = jnp.sum(jnp.where(own_covered, pair_adv[None, :], 0.0), 1)
    ratios = jnp.exp(logits - log_normalizer - own_old)
    bounded = jnp.clip(ratios, 1.0 - clip_low, 1.0 + clip_high)
    objective = jnp.where(own_occupied, jnp.minimum(ratios * token_adv, bounded * token_adv), 0.0)
    loss_sum, counted = (
        over_axes(jnp.sum(objective), ROW_COL_MP),
        over_axes(jnp.sum(own_occupied.astype(jnp.float32)), ROW_COL_MP),
    )
    return (objective, -loss_sum / counted)


def solution(mesh):
    finer = Mesh(
        mesh.devices.reshape(4, 2, mesh.shape["col"], mesh.shape["mp"]),
        ("row_0", "row_1", "col", "mp"),
    )
    placed = (
        P(ROW_COL, "mp"),
        P(ROW_COL),
        P(ROW_COL),
        P(ROW_COL),
        P(ROW_COL),
        P(ROW_COL),
        P(ROW_COL),
        P(),
        P(None, "mp"),
        P("mp"),
        P(None, "mp"),
        P("mp"),
        P(None, "mp"),
        P("mp"),
        P("mp", None),
        P(),
        P(ROW_COL_MP, None),
        P(ROW_COL_MP),
    )
    return jax.shard_map(
        body, mesh=finer, in_specs=placed, out_specs=(P(ROW_COL_MP), P()), check_vma=False
    )
```

profile of v0, /device:TPU:0, one launch (start us, length us, event | category | flops | bytes accessed | tf_op | source)
XLA Modules:
  0.0 239.6 jit_solution(6732604042234698789)
XLA Ops:
  12.6 4.6 %all-to-all-start = ((f32[8,1,4]{2,1,0:T(1,128)}), f32[8,1,4]{2,1,0:T(1,128)S(1)}, u32[]{:S(2)}, u32[]{:S(2)}) async-start(f32[8,1,4]{2,1,0:T(1,128)} %copy.51), calls=%async_computation | async-start | bytes 8192 | tf_op jit(solution)/shard_map/all_to_all | solution.py:127
  17.2 2.3 reshape.258
  20.2 1.5 copy.53
  22.5 4.0 %all-to-all-start.1 = ((bf16[8,128,896]{2,1,0:T(8,128)(2,1)}), bf16[8,128,896]{2,1,0:T(8,128)(2,1)S(1)}, u32[]{:S(2)}, u32[]{:S(2)}) async-start(bf16[8,128,896]{2,1,0:T(8,128)(2,1)} %copy.53), calls=%async_computation.1 | async-start | bytes 3670016 | tf_op jit(solution)/shard_map/all_to_all | solution.py:124
  28.0 22.9 %all-to-all-done.1 = bf16[8,128,896]{2,1,0:T(8,128)(2,1)S(1)} async-done(((bf16[8,128,896]{2,1,0:T(8,128)(2,1)}), bf16[8,128,896]{2,1,0:T(8,128)(2,1)S(1)}, u32[]{:S(2)}, u32[]{:S(2)}) %all-to-all-start.1) | async-done | bytes 1835040 | tf_op jit(solution)/shard_map/all_to_all | solution.py:124
  50.9 2.8 %gather_fusion = bf16[512,896]{1,0:T(8,128)(2,1)} fusion(bf16[1024,896]{1,0:T(8,128)(2,1)S(1)} %bitcast.121, s32[1024]{0:T(1024)S(1)} %pad_clamp_fusion.1), kind=kCustom, calls=%fused_computation | custom fusion | bytes 1837056 | tf_op jit(solution)/shard_map/gather | solution.py:140
  53.6 2.3 broadcast_select_fusion
  58.4 41.8 %all-gather.2.cloned.1.call-done = bf16[512,3584]{1,0:T(8,128)(2,1)} async-done(((bf16[512,896]{1,0:T(8,128)(2,1)}), bf16[512,3584]{1,0:T(8,128)(2,1)}) %all-gather.2.cloned.1.call-update) | async-done | bytes 3670032 | tf_op jit(solution)/shard_map/all_gather | solution.py:141
  100.3 3.0 %fusion = f32[512]{0:T(512)S(1)} fusion(bf16[512,3584]{1,0:T(8,128)(2,1)} %all-gather.2.cloned.1.call-done), kind=kLoop, calls=%fused_computation.5 | loop fusion | flops 5504512 | bytes 3672064 | tf_op jit(solution)/shard_map/reduce_sum | solution.py:143
  103.9 8.1 %convolution_add_fusion = f32[512,896]{1,0:T(8,128)} fusion(bf16[3584,896]{1,0:T(8,128)(2,1)} %param.26, f32[896]{0:T(1024)S(1)} %convert_element_type.138, bf16[512,3584]{1,0:T(8,128)(2,1)S(1)} %copy-done.2, f32[3584]{0:T(1024)S(1)} %convert_element_type.132, f32[512]{0:T(512)S(1)} %add_rsqrt_fusion), kind=kOutput, calls=%fused_computation.26 | convolution fusion | flops 3296133120 | bytes 11947520 | tf_op jit(solution)/shard_map/dot_general | solution.py:150
  111.9 1.8 copy.54
  113.8 1.5 fusion.77
  115.2 1.7 copy.67
  116.9 3.0 %copy.68 = f32[512,7,64]{2,0,1:T(8,128)} copy(f32[512,7,64]{0,2,1:T(8,128)} %get-tuple-element.17) | data formatting | bytes 1835008
  119.9 3.9 %fusion.15 = f32[512,1,128]{0,2,1:T(8,128)S(1)} fusion(bf16[3584,128]{1,0:T(8,128)(2,1)} %param.28, f32[128]{0:T(128)} %convert_element_type.136, bf16[512,3584]{1,0:T(8,128)(2,1)} %all-gather.2.cloned.1.call-done, f32[3584]{0:T(1024)} %copy-done.5, f32[512]{0:T(512)} %copy-done.13), kind=kOutput, calls=%fused_computation.29 | convolution fusion | flops 477167616 | bytes 4866560 | tf_op jit(solution)/shard_map/dot_general | solution.py:156
  124.9 2.1 fusion.4
  127.0 3.0 %copy-done.1 = f32[512,512,7]{1,0,2:T(8,128)} copy-done((f32[512,512,7]{1,0,2:T(8,128)}, f32[512,512,7]{1,0,2:T(8,128)S(1)}, u32[]{:S(2)}) %copy-start.1) | copy-done | bytes 7340056
  130.0 1.6 fusion.3
  131.6 7.6 %fusion.12 = bf16[128,7,512]{2,0,1:T(8,128)(2,1)S(1)} fusion(f32[7,512]{1,0:T(8,128)S(1)} %fusion.3, f32[7,512]{1,0:T(8,128)S(1)} %get-tuple-element.28, f32[512,512,7]{1,0,2:T(8,128)} %copy-done.1, pred[512,512]{0,1:T(8,128)(4,1)S(1)} %fusion.20, bf16[3584,128]{1,0:T(8,128)(2,1)S(1)} %copy-done, f32[128]{0:T(128)S(1)} %copy-done.23, ...), kind=kOutput, calls=%fused_computation.27 | convolution fusion | flops 956628992 | bytes 13152768 | tf_op jit(solution)/shard_map/kgqe,ekd->qkgd/dot_general | solution.py:179
  139.2 8.3 %convolution_convert_fusion.1 = bf16[512,3584]{1,0:T(8,128)(2,1)} fusion(bf16[512,896]{0,1:T(8,128)(2,1)S(1)} %bitcast.130, bf16[896,3584]{1,0:T(8,128)(2,1)} %param.32), kind=kOutput, calls=%fused_computation.12 | convolution fusion | flops 3290169344 | bytes 11010048 | tf_op jit(solution)/shard_map/dot_general | solution.py:184
  148.9 4.3 %all-to-all-start.2 = ((f32[8,1,128]{2,1,0:T(1,128)}), f32[8,1,128]{2,1,0:T(1,128)S(1)}, u32[]{:S(2)}, u32[]{:S(2)}) async-start(f32[8,1,128]{2,1,0:T(1,128)} %bitcast.34), calls=%async_computation.3 | async-start | bytes 8192 | tf_op jit(solution)/shard_map/all_to_all | solution.py:126
  153.7 4.7 %all-to-all-done.2 = f32[8,1,128]{2,1,0:T(1,128)S(1)} async-done(((f32[8,1,128]{2,1,0:T(1,128)}), f32[8,1,128]{2,1,0:T(1,128)S(1)}, u32[]{:S(2)}, u32[]{:S(2)}) %all-to-all-start.2) | async-done | bytes 4128 | tf_op jit(solution)/shard_map/all_to_all | solution.py:126
  159.0 5.4 %all-to-all-start.3 = ((f32[32,1,64]{2,1,0:T(1,128)}), f32[32,1,64]{2,1,0:T(1,128)S(1)}, u32[]{:S(2)}, u32[]{:S(2)}) async-start(f32[32,1,64]{2,1,0:T(1,128)} %broadcast_in_dim.65), calls=%async_computation.4 | async-start | bytes 32768 | tf_op jit(solution)/shard_map/all_to_all | solution.py:22
  165.5 6.4 %all-to-all-done.3 = f32[32,1,64]{2,1,0:T(1,128)S(1)} async-done(((f32[32,1,64]{2,1,0:T(1,128)}), f32[32,1,64]{2,1,0:T(1,128)S(1)}, u32[]{:S(2)}, u32[]{:S(2)}) %all-to-all-start.3) | async-done | bytes 8224 | tf_op jit(solution)/shard_map/all_to_all | solution.py:22
  173.0 17.5 %reduce-scatter.2.cloned.1.call-done = bf16[128,3584]{1,0:T(8,128)(2,1)} async-done(((bf16[512,3584]{1,0:T(8,128)(2,1)}), bf16[128,3584]{1,0:T(8,128)(2,1)}) %reduce-scatter.2.cloned.1.call-update) | async-done | bytes 917520 | tf_op jit(solution)/shard_map/reduce_scatter | solution.py:183
  190.5 1.8 fusion.8
  192.3 2.1 fusion.11
  194.4 1.2 fusion.76
  195.6 11.2 %all-reduce.2 = (f32[]{:T(128)}, f32[]{:T(128)}) all-reduce(f32[]{:T(128)} %get-tuple-element.13, f32[]{:T(128)} %get-tuple-element.27), channel_id=1, replica_groups=mesh['row_0'=4,'row_1'=2,'col'=4,'mp'=4] {'row_0'}, use_global_device_ids=true, to_apply=%region_14.15 | all-reduce | flops 2 | bytes 16 | tf_op jit(solution)/shard_map/psum | solution.py:40
  206.8 3.1 %all-reduce.3 = (f32[]{:T(128)}, f32[]{:T(128)}) all-reduce(f32[]{:T(128)} %get-tuple-element.9, f32[]{:T(128)} %get-tuple-element.10), channel_id=1, replica_groups=mesh['row_0'=4,'row_1'=2,'col'=4,'mp'=4] {'row_1'}, use_global_device_ids=true, to_apply=%region_15.16 | all-reduce | flops 2 | bytes 16 | tf_op jit(solution)/shard_map/psum | solution.py:40
  209.9 11.3 %all-reduce.1 = (f32[]{:T(128)}, f32[]{:T(128)}) all-reduce(f32[]{:T(128)} %get-tuple-element.11, f32[]{:T(128)} %get-tuple-element.12), channel_id=1, replica_groups=mesh['row_0'=4,'row_1'=2,'col'=4,'mp'=4] {'col'}, use_global_device_ids=true, to_apply=%region_16.17 | all-reduce | flops 2 | bytes 16 | tf_op jit(solution)/shard_map/psum | solution.py:40
  221.2 9.2 %all-reduce = (f32[]{:T(128)}, f32[]{:T(128)}) all-reduce(f32[]{:T(128)} %get-tuple-element.7, f32[]{:T(128)} %get-tuple-element.8), channel_id=1, replica_groups=mesh['row_0'=4,'row_1'=2,'col'=4,'mp'=4] {'mp'}, use_global_device_ids=true, to_apply=%region_17.18 | all-reduce | flops 2 | bytes 16 | tf_op jit(solution)/shard_map/psum | solution.py:40
  (95 shorter events, 17.0 us)
Async XLA Ops:
  7.2 124.4 %copy-start = (bf16[3584,128]{1,0:T(8,128)(2,1)S(1)}, bf16[3584,128]{1,0:T(8,128)(2,1)}, u32[]{:S(2)}) copy-start(bf16[3584,128]{1,0:T(8,128)(2,1)} %param.30) | copy-start | bytes 2752516
  8.8 11.4 %copy-start.15 = (s32[8]{0:T(128)}, s32[8]{0:T(128)S(1)}, u32[]{:S(2)}) copy-start(s32[8]{0:T(128)S(1)} %fusion.84) | copy-start | bytes 100
  12.6 9.9 %all-to-all-start = ((f32[8,1,4]{2,1,0:T(1,128)}), f32[8,1,4]{2,1,0:T(1,128)S(1)}, u32[]{:S(2)}, u32[]{:S(2)}) async-start(f32[8,1,4]{2,1,0:T(1,128)} %copy.51), calls=%async_computation | async-start | bytes 8192 | tf_op jit(solution)/shard_map/all_to_all | solution.py:127
  22.5 28.4 %all-to-all-start.1 = ((bf16[8,128,896]{2,1,0:T(8,128)(2,1)}), bf16[8,128,896]{2,1,0:T(8,128)(2,1)S(1)}, u32[]{:S(2)}, u32[]{:S(2)}) async-start(bf16[8,128,896]{2,1,0:T(8,128)(2,1)} %copy.53), calls=%async_computation.1 | async-start | bytes 3670016 | tf_op jit(solution)/shard_map/all_to_all | solution.py:124
  26.5 73.8 %all-gather.2.cloned.1.call-start = ((), (), s32[]{:S(2)}) async-start(), calls=%async_computation.5 | async-start | bytes 4587520 | tf_op jit(solution)/shard_map/all_gather | solution.py:141
  50.9 5.1 %copy-start.7 = (bf16[3584]{0:T(1024)(128)(2,1)S(1)}, bf16[3584]{0:T(1024)(128)(2,1)}, u32[]{:S(2)}) copy-start(bf16[3584]{0:T(1024)(128)(2,1)} %param.25) | copy-start | bytes 21508
  50.9 5.1 %copy-start.12 = (bf16[896]{0:T(1024)(128)(2,1)S(1)}, bf16[896]{0:T(1024)(128)(2,1)}, u32[]{:S(2)}) copy-start(bf16[896]{0:T(1024)(128)(2,1)} %param.27) | copy-start | bytes 5380
  50.9 5.2 %copy-start.19 = (bf16[128]{0:T(256)(128)(2,1)S(1)}, bf16[128]{0:T(256)(128)(2,1)}, u32[]{:S(2)}) copy-start(bf16[128]{0:T(256)(128)(2,1)} %param.29) | copy-start | bytes 772
  50.9 5.8 %copy-start.20 = (bf16[128]{0:T(256)(128)(2,1)S(1)}, bf16[128]{0:T(256)(128)(2,1)}, u32[]{:S(2)}) copy-start(bf16[128]{0:T(256)(128)(2,1)} %param.31) | copy-start | bytes 772
  55.9 134.5 %reduce-scatter.2.cloned.1.call-start = ((), (), s32[]{:S(2)}) async-start(), calls=%async_computation.6 | async-start | bytes 4587520 | tf_op jit(solution)/shard_map/reduce_scatter | solution.py:183
  56.0 47.2 %copy-start.5 = (f32[3584]{0:T(1024)}, f32[3584]{0:T(1024)S(1)}, u32[]{:S(2)}) copy-start(f32[3584]{0:T(1024)S(1)} %convert_element_type.132) | copy-start | bytes 43012
  57.2 1.2 copy-start.10
  100.3 3.6 %copy-start.2 = (bf16[512,3584]{1,0:T(8,128)(2,1)S(1)}, bf16[512,3584]{1,0:T(8,128)(2,1)}, u32[]{:S(2)}) copy-start(bf16[512,3584]{1,0:T(8,128)(2,1)} %all-gather.2.cloned.1.call-done) | copy-start | bytes 11010052
  103.3 0.6 copy-start.13
  119.9 3.9 %copy-start.11 = (f32[64]{0:T(128)S(1)}, f32[64]{0:T(128)}, u32[]{:S(2)}) copy-start(f32[64]{0:T(128)} %copy-done.10) | copy-start | bytes 772
  119.9 4.5 %copy-start.3 = (f32[512,7,64]{2,0,1:T(8,128)S(1)}, f32[512,7,64]{2,0,1:T(8,128)}, u32[]{:S(2)}) copy-start(f32[512,7,64]{2,0,1:T(8,128)} %copy.68) | copy-start | bytes 2752516
  127.0 3.0 %copy-start.1 = (f32[512,512,7]{1,0,2:T(8,128)}, f32[512,512,7]{1,0,2:T(8,128)S(1)}, u32[]{:S(2)}) copy-start(f32[512,512,7]{1,0,2:T(8,128)S(1)} %get-tuple-element.29) | copy-start | bytes 22020100
  130.0 1.6 copy-start.6
  130.0 1.6 copy-start.14
  130.0 1.6 copy-start.23
  147.5 0.7 copy-start.9
  147.5 0.7 copy-start.16
  147.5 5.7 %copy-start.8 = (bf16[3584]{0:T(1024)(128)(2,1)S(1)}, bf16[3584]{0:T(1024)(128)(2,1)}, u32[]{:S(2)}) copy-start(bf16[3584]{0:T(1024)(128)(2,1)} %param.33) | copy-start | bytes 21508
  147.5 5.7 %copy-start.21 = (s32[8]{0:T(128)S(1)}, s32[8]{0:T(128)}, u32[]{:S(2)}) copy-start(s32[8]{0:T(128)} %param.24) | copy-start | bytes 100
  147.5 5.7 %copy-start.22 = (f32[8]{0:T(128)S(1)}, f32[8]{0:T(128)}, u32[]{:S(2)}) copy-start(f32[8]{0:T(128)} %param.20) | copy-start | bytes 100
  147.5 24.4 %copy-start.18 = (s32[8]{0:T(128)S(1)}, s32[8]{0:T(128)}, u32[]{:S(2)}) copy-start(s32[8]{0:T(128)} %get-tuple-element.23) | copy-start | bytes 100
  147.5 44.8 %copy-start.4 = (bf16[128,3584]{1,0:T(8,128)(2,1)S(1)}, bf16[128,3584]{1,0:T(8,128)(2,1)}, u32[]{:S(2)}) copy-start(bf16[128,3584]{1,0:T(8,128)(2,1)} %param.34) | copy-start | bytes 2752516
  148.1 46.3 %copy-start.17 = (f32[128]{0:T(128)S(1)}, f32[128]{0:T(128)}, u32[]{:S(2)}) copy-start(f32[128]{0:T(128)} %param.35) | copy-start | bytes 1540
  148.9 9.6 %all-to-all-start.2 = ((f32[8,1,128]{2,1,0:T(1,128)}), f32[8,1,128]{2,1,0:T(1,128)S(1)}, u32[]{:S(2)}, u32[]{:S(2)}) async-start(f32[8,1,128]{2,1,0:T(1,128)} %bitcast.34), calls=%async_computation.3 | async-start | bytes 8192 | tf_op jit(solution)/shard_map/all_to_all | solution.py:126
  159.0 12.8 %all-to-all-start.3 = ((f32[32,1,64]{2,1,0:T(1,128)}), f32[32,1,64]{2,1,0:T(1,128)S(1)}, u32[]{:S(2)}, u32[]{:S(2)}) async-start(f32[32,1,64]{2,1,0:T(1,128)} %broadcast_in_dim.65), calls=%async_computation.4 | async-start | bytes 32768 | tf_op jit(solution)/shard_map/all_to_all | solution.py:22
Sparse Core Ops, SparseCore 0:
  56.1 44.1 all-gather.1
  147.7 42.7 reduce-scatter.1
where the time goes:
time: 240 us
  waiting for transfers between devices  94.2 us (39%)
  matrix products  35.1 us (15%)
  blocking collectives  34.8 us (14%)
  local copies, waits for them, and re-layouts  21.2 us (9%)
  other arithmetic  19.2 us (8%)
  starting transfers between devices  18.4 us (8%)
  between operations  16.8 us (7%)
    all_gather x1, waiting for transfers between devices, body(): gathered = lax.all_gather(packed, 'mp', axis=1, tiled=True)  41.8 us
    psum x4, blocking collectives, over_axes(): value = lax.psum(value, axis)  34.8 us
    all_to_all x1, waiting for transfers between devices, body(): lax.all_to_all(send_rows, ROW, split_axis=0, concat_axis=0, tiled=True)  22.9 us
    reduce_scatter x1, waiting for transfers between devices, body(): lax.psum_scatter(jnp.dot(pieces, w_out, preferred_element_type=jnp.float3...  17.5 us
    unnamed x50, local copies, waits for them, and re-layouts  8.94 us
    dot_general x1, matrix products, body(): jnp.dot(pieces, w_out, preferred_element_type=jnp.float32)  8.28 us
    dot_general x1, matrix products, body(): jnp.dot(normed, w_query, preferred_element_type=jnp.float32)  8.08 us
    dot_general x1, matrix products, body(): jnp.einsum('kgqe,ekd->qkgd', weights, value_rows, preferred_element_type=...  7.58 us
  transfers between devices with their start and end apart: 6, of which 6 were waited for; matrix products, arithmetic and copies ran while one was open for 5% of the time, Pallas kernels for 0%

commit v1 on v0

--- a/solution.py
+++ b/solution.py
@@ -37,7 +37,8 @@
 
 def over_axes(value, axes):
     for axis in axes:
-        value = lax.psum(value, axis)
+        blocks = lax.all_gather(value, axis, axis=0, tiled=False)
+        value = blocks.sum(axis=0)
     return value
 
 

time: 240 us -> 256 us (1.067)
  local copies, waits for them, and re-layouts: 21.2 us -> 35.1 us
  other arithmetic: 19.2 us -> 24.1 us
  blocking collectives: 34.8 us -> 32.1 us
    psum x4 -> x0, blocking collectives: 34.8 us -> none  [over_axes(): value = lax.psum(value, axis)]
    unnamed x0 -> x4, blocking collectives: none -> 32.1 us
    unnamed x50 -> x78, local copies, waits for them, and re-layouts: 8.94 us -> 22.9 us
    reduce_sum x0 -> x8, other arithmetic: none -> 4.79 us  [over_axes(): value = blocks.sum(axis=0)]
where the time goes in v1:
time: 256 us; the launch traced here: 255 us
  waiting for transfers between devices  93.3 us (36%)
  local copies, waits for them, and re-layouts  35.1 us (14%)
  matrix products  35.1 us (14%)
  blocking collectives  32.1 us (13%)
  other arithmetic  24.1 us (9%)
  starting transfers between devices  18.6 us (7%)
  between operations  16.9 us (7%)
    all_gather x1, waiting for transfers between devices, body(): gathered = lax.all_gather(packed, 'mp', axis=1, tiled=True)  41.8 us
    unnamed x4, blocking collectives  32.1 us
    all_to_all x1, waiting for transfers between devices, body(): lax.all_to_all(send_rows, ROW, split_axis=0, concat_axis=0, tiled=True)  22.9 us
    unnamed x78, local copies, waits for them, and re-layouts  22.9 us
    reduce_scatter x1, waiting for transfers between devices, body(): lax.psum_scatter(jnp.dot(pieces, w_out, preferred_element_type=jnp.float3...  17.3 us
    dot_general x1, matrix products, body(): jnp.dot(pieces, w_out, preferred_element_type=jnp.float32)  8.28 us
    dot_general x1, matrix products, body(): jnp.dot(normed, w_query, preferred_element_type=jnp.float32)  8.08 us
    dot_general x1, matrix products, body(): jnp.einsum('kgqe,ekd->qkgd', weights, value_rows, preferred_element_type=...  7.58 us
  transfers between devices with their start and end apart: 6, of which 6 were waited for; matrix products, arithmetic and copies ran while one was open for 5% of the time, Pallas kernels for 0%

profile of v1, /device:TPU:0, one launch (start us, length us, event | category | flops | bytes accessed | tf_op | source)
XLA Modules:
  0.0 255.2 jit_solution(8067595644753070933)
XLA Ops:
  12.6 4.6 %all-to-all-start = ((f32[8,1,4]{2,1,0:T(1,128)}), f32[8,1,4]{2,1,0:T(1,128)S(1)}, u32[]{:S(2)}, u32[]{:S(2)}) async-start(f32[8,1,4]{2,1,0:T(1,128)} %copy.51), calls=%async_computation | async-start | bytes 8192 | tf_op jit(solution)/shard_map/all_to_all | solution.py:128
  17.2 2.3 reshape.258
  20.2 1.5 copy.53
  22.5 4.0 %all-to-all-start.1 = ((bf16[8,128,896]{2,1,0:T(8,128)(2,1)}), bf16[8,128,896]{2,1,0:T(8,128)(2,1)S(1)}, u32[]{:S(2)}, u32[]{:S(2)}) async-start(bf16[8,128,896]{2,1,0:T(8,128)(2,1)} %copy.53), calls=%async_computation.1 | async-start | bytes 3670016 | tf_op jit(solution)/shard_map/all_to_all | solution.py:125
  28.0 22.9 %all-to-all-done.1 = bf16[8,128,896]{2,1,0:T(8,128)(2,1)S(1)} async-done(((bf16[8,128,896]{2,1,0:T(8,128)(2,1)}), bf16[8,128,896]{2,1,0:T(8,128)(2,1)S(1)}, u32[]{:S(2)}, u32[]{:S(2)}) %all-to-all-start.1) | async-done | bytes 1835040 | tf_op jit(solution)/shard_map/all_to_all | solution.py:125
  50.9 2.8 %gather_fusion = bf16[512,896]{1,0:T(8,128)(2,1)} fusion(bf16[1024,896]{1,0:T(8,128)(2,1)S(1)} %bitcast.133, s32[1024]{0:T(1024)S(1)} %pad_clamp_fusion.1), kind=kCustom, calls=%fused_computation | custom fusion | bytes 1837056 | tf_op jit(solution)/shard_map/gather | solution.py:141
  53.6 2.3 broadcast_select_fusion
  58.4 41.8 %all-gather.2.cloned.1.call-done = bf16[512,3584]{1,0:T(8,128)(2,1)} async-done(((bf16[512,896]{1,0:T(8,128)(2,1)}), bf16[512,3584]{1,0:T(8,128)(2,1)}) %all-gather.2.cloned.1.call-update) | async-done | bytes 3670032 | tf_op jit(solution)/shard_map/all_gather | solution.py:142
  100.3 3.0 %fusion = f32[512]{0:T(512)S(1)} fusion(bf16[512,3584]{1,0:T(8,128)(2,1)} %all-gather.2.cloned.1.call-done), kind=kLoop, calls=%fused_computation.5 | loop fusion | flops 5504512 | bytes 3672064 | tf_op jit(solution)/shard_map/reduce_sum | solution.py:144
  103.9 8.1 %convolution_add_fusion = f32[512,896]{1,0:T(8,128)} fusion(bf16[3584,896]{1,0:T(8,128)(2,1)} %param.26, f32[896]{0:T(1024)S(1)} %convert_element_type.138, bf16[512,3584]{1,0:T(8,128)(2,1)S(1)} %copy-done.2, f32[3584]{0:T(1024)S(1)} %convert_element_type.132, f32[512]{0:T(512)S(1)} %add_rsqrt_fusion), kind=kOutput, calls=%fused_computation.26 | convolution fusion | flops 3296133120 | bytes 11947520 | tf_op jit(solution)/shard_map/dot_general | solution.py:151
  111.9 1.8 copy.54
  113.8 1.5 fusion.77
  115.2 1.7 copy.67
  116.9 3.0 %copy.68 = f32[512,7,64]{2,0,1:T(8,128)} copy(f32[512,7,64]{0,2,1:T(8,128)} %get-tuple-element.17) | data formatting | bytes 1835008
  119.9 3.9 %fusion.15 = f32[512,1,128]{0,2,1:T(8,128)S(1)} fusion(bf16[3584,128]{1,0:T(8,128)(2,1)} %param.28, f32[128]{0:T(128)} %convert_element_type.136, bf16[512,3584]{1,0:T(8,128)(2,1)} %all-gather.2.cloned.1.call-done, f32[3584]{0:T(1024)} %copy-done.5, f32[512]{0:T(512)} %copy-done.13), kind=kOutput, calls=%fused_computation.29 | convolution fusion | flops 477167616 | bytes 4866560 | tf_op jit(solution)/shard_map/dot_general | solution.py:157
  124.9 2.1 fusion.4
  127.0 3.0 %copy-done.1 = f32[512,512,7]{1,0,2:T(8,128)} copy-done((f32[512,512,7]{1,0,2:T(8,128)}, f32[512,512,7]{1,0,2:T(8,128)S(1)}, u32[]{:S(2)}) %copy-start.1) | copy-done | bytes 7340056
  130.0 1.6 fusion.3
  131.6 7.6 %fusion.12 = bf16[128,7,512]{2,0,1:T(8,128)(2,1)S(1)} fusion(f32[7,512]{1,0:T(8,128)S(1)} %fusion.3, f32[7,512]{1,0:T(8,128)S(1)} %get-tuple-element.28, f32[512,512,7]{1,0,2:T(8,128)} %copy-done.1, pred[512,512]{0,1:T(8,128)(4,1)S(1)} %fusion.20, bf16[3584,128]{1,0:T(8,128)(2,1)S(1)} %copy-done, f32[128]{0:T(128)S(1)} %copy-done.27, ...), kind=kOutput, calls=%fused_computation.27 | convolution fusion | flops 956628992 | bytes 13152768 | tf_op jit(solution)/shard_map/kgqe,ekd->qkgd/dot_general | solution.py:180
  139.2 8.3 %convolution_convert_fusion.1 = bf16[512,3584]{1,0:T(8,128)(2,1)} fusion(bf16[512,896]{0,1:T(8,128)(2,1)S(1)} %bitcast.142, bf16[896,3584]{1,0:T(8,128)(2,1)} %param.32), kind=kOutput, calls=%fused_computation.12 | convolution fusion | flops 3290169344 | bytes 11010048 | tf_op jit(solution)/shard_map/dot_general | solution.py:185
  148.9 4.3 %all-to-all-start.2 = ((f32[8,1,128]{2,1,0:T(1,128)}), f32[8,1,128]{2,1,0:T(1,128)S(1)}, u32[]{:S(2)}, u32[]{:S(2)}) async-start(f32[8,1,128]{2,1,0:T(1,128)} %bitcast.34), calls=%async_computation.3 | async-start | bytes 8192 | tf_op jit(solution)/shard_map/all_to_all | solution.py:127
  154.4 4.1 %all-to-all-done.2 = f32[8,1,128]{2,1,0:T(1,128)S(1)} async-done(((f32[8,1,128]{2,1,0:T(1,128)}), f32[8,1,128]{2,1,0:T(1,128)S(1)}, u32[]{:S(2)}, u32[]{:S(2)}) %all-to-all-start.2) | async-done | bytes 4128 | tf_op jit(solution)/shard_map/all_to_all | solution.py:127
  159.1 5.6 %all-to-all-start.3 = ((f32[32,1,64]{2,1,0:T(1,128)}), f32[32,1,64]{2,1,0:T(1,128)S(1)}, u32[]{:S(2)}, u32[]{:S(2)}) async-start(f32[32,1,64]{2,1,0:T(1,128)} %broadcast_in_dim.65), calls=%async_computation.4 | async-start | bytes 32768 | tf_op jit(solution)/shard_map/all_to_all | solution.py:22
  165.7 6.4 %all-to-all-done.3 = f32[32,1,64]{2,1,0:T(1,128)S(1)} async-done(((f32[32,1,64]{2,1,0:T(1,128)}), f32[32,1,64]{2,1,0:T(1,128)S(1)}, u32[]{:S(2)}, u32[]{:S(2)}) %all-to-all-start.3) | async-done | bytes 8224 | tf_op jit(solution)/shard_map/all_to_all | solution.py:22
  173.2 17.3 %reduce-scatter.2.cloned.1.call-done = bf16[128,3584]{1,0:T(8,128)(2,1)} async-done(((bf16[512,3584]{1,0:T(8,128)(2,1)}), bf16[128,3584]{1,0:T(8,128)(2,1)}) %reduce-scatter.2.cloned.1.call-update) | async-done | bytes 917520 | tf_op jit(solution)/shard_map/reduce_scatter | solution.py:184
  190.5 1.8 fusion.8
  192.4 2.1 fusion.11
  197.2 1.5 dynamic-update-slice.4
  199.3 10.4 %all-reduce.10 = (f32[4]{0:T(128)S(1)}, f32[4]{0:T(128)S(1)}) all-reduce(f32[4]{0:T(128)S(1)} %dynamic-update-slice, f32[4]{0:T(128)S(1)} %dynamic-update-slice.4), channel_id=1, replica_groups=mesh['row_0'=4,'row_1'=2,'col'=4,'mp'=4] {'row_0'}, use_global_device_ids=true, to_apply=%add | all-reduce | flops 8 | bytes 64
  214.4 2.4 all-reduce.11
  221.5 10.6 %all-reduce.9 = (f32[4]{0:T(128)S(1)}, f32[4]{0:T(128)S(1)}) all-reduce(f32[4]{0:T(128)S(1)} %dynamic-update-slice.2, f32[4]{0:T(128)S(1)} %dynamic-update-slice.6), channel_id=1, replica_groups=mesh['row_0'=4,'row_1'=2,'col'=4,'mp'=4] {'col'}, use_global_device_ids=true, to_apply=%add.2 | all-reduce | flops 8 | bytes 64
  236.1 8.6 %all-reduce.8 = (f32[4]{0:T(128)S(1)}, f32[4]{0:T(128)S(1)}) all-reduce(f32[4]{0:T(128)S(1)} %dynamic-update-slice.3, f32[4]{0:T(128)S(1)} %dynamic-update-slice.7), channel_id=1, replica_groups=mesh['row_0'=4,'row_1'=2,'col'=4,'mp'=4] {'mp'}, use_global_device_ids=true, to_apply=%add.3 | all-reduce | flops 8 | bytes 64
  (131 shorter events, 35.5 us)
Async XLA Ops:
  7.2 124.4 %copy-start = (bf16[3584,128]{1,0:T(8,128)(2,1)S(1)}, bf16[3584,128]{1,0:T(8,128)(2,1)}, u32[]{:S(2)}) copy-start(bf16[3584,128]{1,0:T(8,128)(2,1)} %param.30) | copy-start | bytes 2752516
  8.8 11.4 %copy-start.15 = (s32[8]{0:T(128)}, s32[8]{0:T(128)S(1)}, u32[]{:S(2)}) copy-start(s32[8]{0:T(128)S(1)} %fusion.84) | copy-start | bytes 100
  12.6 9.9 %all-to-all-start = ((f32[8,1,4]{2,1,0:T(1,128)}), f32[8,1,4]{2,1,0:T(1,128)S(1)}, u32[]{:S(2)}, u32[]{:S(2)}) async-start(f32[8,1,4]{2,1,0:T(1,128)} %copy.51), calls=%async_computation | async-start | bytes 8192 | tf_op jit(solution)/shard_map/all_to_all | solution.py:128
  22.5 28.4 %all-to-all-start.1 = ((bf16[8,128,896]{2,1,0:T(8,128)(2,1)}), bf16[8,128,896]{2,1,0:T(8,128)(2,1)S(1)}, u32[]{:S(2)}, u32[]{:S(2)}) async-start(bf16[8,128,896]{2,1,0:T(8,128)(2,1)} %copy.53), calls=%async_computation.1 | async-start | bytes 3670016 | tf_op jit(solution)/shard_map/all_to_all | solution.py:125
  26.5 73.8 %all-gather.2.cloned.1.call-start = ((), (), s32[]{:S(2)}) async-start(), calls=%async_computation.5 | async-start | bytes 4587520 | tf_op jit(solution)/shard_map/all_gather | solution.py:142
  50.9 5.1 %copy-start.7 = (bf16[3584]{0:T(1024)(128)(2,1)S(1)}, bf16[3584]{0:T(1024)(128)(2,1)}, u32[]{:S(2)}) copy-start(bf16[3584]{0:T(1024)(128)(2,1)} %param.25) | copy-start | bytes 21508
  50.9 5.1 %copy-start.12 = (bf16[896]{0:T(1024)(128)(2,1)S(1)}, bf16[896]{0:T(1024)(128)(2,1)}, u32[]{:S(2)}) copy-start(bf16[896]{0:T(1024)(128)(2,1)} %param.27) | copy-start | bytes 5380
  50.9 5.2 %copy-start.19 = (bf16[128]{0:T(256)(128)(2,1)S(1)}, bf16[128]{0:T(256)(128)(2,1)}, u32[]{:S(2)}) copy-start(bf16[128]{0:T(256)(128)(2,1)} %param.29) | copy-start | bytes 772
  50.9 5.8 %copy-start.20 = (bf16[128]{0:T(256)(128)(2,1)S(1)}, bf16[128]{0:T(256)(128)(2,1)}, u32[]{:S(2)}) copy-start(bf16[128]{0:T(256)(128)(2,1)} %param.31) | copy-start | bytes 772
  55.9 134.6 %reduce-scatter.2.cloned.1.call-start = ((), (), s32[]{:S(2)}) async-start(), calls=%async_computation.6 | async-start | bytes 4587520 | tf_op jit(solution)/shard_map/reduce_scatter | solution.py:184
  56.0 47.2 %copy-start.5 = (f32[3584]{0:T(1024)}, f32[3584]{0:T(1024)S(1)}, u32[]{:S(2)}) copy-start(f32[3584]{0:T(1024)S(1)} %convert_element_type.132) | copy-start | bytes 43012
  57.2 1.2 copy-start.10
  100.3 3.6 %copy-start.2 = (bf16[512,3584]{1,0:T(8,128)(2,1)S(1)}, bf16[512,3584]{1,0:T(8,128)(2,1)}, u32[]{:S(2)}) copy-start(bf16[512,3584]{1,0:T(8,128)(2,1)} %all-gather.2.cloned.1.call-done) | copy-start | bytes 11010052
  119.9 3.9 %copy-start.11 = (f32[64]{0:T(128)S(1)}, f32[64]{0:T(128)}, u32[]{:S(2)}) copy-start(f32[64]{0:T(128)} %copy-done.10) | copy-start | bytes 772
  119.9 4.5 %copy-start.3 = (f32[512,7,64]{2,0,1:T(8,128)S(1)}, f32[512,7,64]{2,0,1:T(8,128)}, u32[]{:S(2)}) copy-start(f32[512,7,64]{2,0,1:T(8,128)} %copy.68) | copy-start | bytes 2752516
  127.0 3.0 %copy-start.1 = (f32[512,512,7]{1,0,2:T(8,128)}, f32[512,512,7]{1,0,2:T(8,128)S(1)}, u32[]{:S(2)}) copy-start(f32[512,512,7]{1,0,2:T(8,128)S(1)} %get-tuple-element.29) | copy-start | bytes 22020100
  130.0 1.6 copy-start.6
  130.0 1.6 copy-start.14
  130.0 1.6 copy-start.27
  147.5 0.7 copy-start.16
  147.5 5.7 %copy-start.8 = (bf16[3584]{0:T(1024)(128)(2,1)S(1)}, bf16[3584]{0:T(1024)(128)(2,1)}, u32[]{:S(2)}) copy-start(bf16[3584]{0:T(1024)(128)(2,1)} %param.33) | copy-start | bytes 21508
  147.5 5.7 %copy-start.26 = (u32[128]{0:T(128)S(1)}, u32[128]{0:T(128)}, u32[]{:S(2)}) copy-start(u32[128]{0:T(128)} %constant.74) | copy-start | bytes 1540
  147.5 6.4 %copy-start.21 = (s32[8]{0:T(128)S(1)}, s32[8]{0:T(128)}, u32[]{:S(2)}) copy-start(s32[8]{0:T(128)} %param.24) | copy-start | bytes 100
  147.5 6.4 %copy-start.22 = (f32[8]{0:T(128)S(1)}, f32[8]{0:T(128)}, u32[]{:S(2)}) copy-start(f32[8]{0:T(128)} %param.20) | copy-start | bytes 100
  147.5 24.6 %copy-start.18 = (s32[8]{0:T(128)S(1)}, s32[8]{0:T(128)}, u32[]{:S(2)}) copy-start(s32[8]{0:T(128)} %get-tuple-element.23) | copy-start | bytes 100
  147.5 44.8 %copy-start.4 = (bf16[128,3584]{1,0:T(8,128)(2,1)S(1)}, bf16[128,3584]{1,0:T(8,128)(2,1)}, u32[]{:S(2)}) copy-start(bf16[128,3584]{1,0:T(8,128)(2,1)} %param.34) | copy-start | bytes 2752516
  148.1 46.3 %copy-start.17 = (f32[128]{0:T(128)S(1)}, f32[128]{0:T(128)}, u32[]{:S(2)}) copy-start(f32[128]{0:T(128)} %param.35) | copy-start | bytes 1540
  148.1 50.5 %copy-start.25 = (u32[128]{0:T(128)S(1)}, u32[128]{0:T(128)}, u32[]{:S(2)}) copy-start(u32[128]{0:T(128)} %constant.79) | copy-start | bytes 1540
  148.1 65.6 %copy-start.24 = (u32[128]{0:T(128)S(1)}, u32[128]{0:T(128)}, u32[]{:S(2)}) copy-start(u32[128]{0:T(128)} %constant.84) | copy-start | bytes 1540
  148.2 72.7 %copy-start.23 = (u32[128]{0:T(128)S(1)}, u32[128]{0:T(128)}, u32[]{:S(2)}) copy-start(u32[128]{0:T(128)} %constant.89) | copy-start | bytes 1540
  148.9 9.6 %all-to-all-start.2 = ((f32[8,1,128]{2,1,0:T(1,128)}), f32[8,1,128]{2,1,0:T(1,128)S(1)}, u32[]{:S(2)}, u32[]{:S(2)}) async-start(f32[8,1,128]{2,1,0:T(1,128)} %bitcast.34), calls=%async_computation.3 | async-start | bytes 8192 | tf_op jit(solution)/shard_map/all_to_all | solution.py:127
  159.1 13.0 %all-to-all-start.3 = ((f32[32,1,64]{2,1,0:T(1,128)}), f32[32,1,64]{2,1,0:T(1,128)S(1)}, u32[]{:S(2)}, u32[]{:S(2)}) async-start(f32[32,1,64]{2,1,0:T(1,128)} %broadcast_in_dim.65), calls=%async_computation.4 | async-start | bytes 32768 | tf_op jit(solution)/shard_map/all_to_all | solution.py:22
  (2 other events, 1.3 us)
Sparse Core Ops, SparseCore 0:
  56.1 44.1 all-gather.1
  147.7 42.7 reduce-scatter.1
